TPU v7x, 32 devices: a whole 2x2x4 slice. The times are simulated.
32 devices in a mesh: groups: 2 (over x), docs: 16 (over z, y, core).
Axes of the slice: x: 2, y: 2, z: 4, core: 2. Of those that a mesh axis runs over, the one named last changes fastest.
Arguments:
- sentences: bfloat16 [65536, 1280], P(('groups', 'docs')), parts along dimension 0, may hold values from -10 to 10
- sent_doc: int32 [65536], P('groups'), parts along dimension 0, may hold values from 0 to 2047, never falling along the last dimension, each value on 1 to 32 neighbouring positions
- images: bfloat16 [8192, 1280], P(('groups', 'docs')), parts along dimension 0, may hold values from -30 to 30
- image_owner: int32 [8192, 1], P(('groups', 'docs')), parts along dimension 0, may hold values from 0 to 15, as said below
- anchor: int32 [8192], P(('groups', 'docs')), parts along dimension 0, may hold values from 0 to 2047, as said below
- loader_shard: int32 [8192, 1], P(('groups', 'docs')), parts along dimension 0, may hold values from 0 to 15, as said below
Outputs:
- loaded_images: bfloat16 [16384, 1280], P(('groups', 'docs')), parts along dimension 0
- loaded_text: bfloat16 [16384, 1280], P(('groups', 'docs')), parts along dimension 0
There are 2 independent parts, one for each index of `groups`. A program takes and returns all parts, laid end to end along the dimension named above; each array names one. Nothing has to cross between parts.
Inputs may be any that keep to these rules, and one draw needn't show every extreme that they name: `sent_doc`: documents are runs of 1 to 32 consecutive sentences, ids never falling. `image_owner`: the 256 images of one device name one owner at most 32 times, and some owner exactly 32 times. loader_shard = (a[source device] + b[image_owner]) mod 16 for two permutations a and b of the devices, drawn with the data. So the images of one device name one shard at most 32 times (some exactly 32), and the images that one owner receives from all devices name one shard at most 32 times, all from one source device. `anchor`: the image's document is the document of this sentence of its owner.
All inputs are finite; a program needn't handle non-finite values.
Results may differ from a plain program's by a relative error of at most 0.0048.
Values may be sent and summed in bfloat16 or wider, within the bound.
A program may use at most 64 MiB of HBM per device.

v0:
```python
import jax
import jax.numpy as jnp
from jax import lax
from jax.sharding import PartitionSpec as P

MOST_SENT = 32


def extended_2(shard, sides, width):
    for axis, dim in sides:
        peers, length = (lax.axis_size(axis), shard.shape[dim])
        up = [(i, (i + 1) % peers) for i in range(peers - 1)]
        down = [(j, i) for i, j in up]
        last = lax.slice_in_dim(shard, length - width, length, axis=dim)
        first = lax.slice_in_dim(shard, 0, width, axis=dim)
        before = lax.ppermute(last, axis, up)
        after = lax.ppermute(first, axis, down)
        shard = jnp.concatenate([before, shard, after], axis=dim)
    return shard


def ranks_of(targets, members):
    labels = jnp.arange(members, dtype=jnp.int32)
    onehot = (targets[:, None] == labels[None, :]).astype(jnp.int32)
    return jnp.sum((jnp.cumsum(onehot, axis=0) - 1) * onehot, axis=1)


def slot_table(targets, members, capacity):
    places = targets * capacity + ranks_of(targets, members)
    slot_ids = jnp.arange(members * capacity, dtype=jnp.int32)
    return slot_ids[:, None] == places[None, :]


def spread_values(table, values):
    return jnp.sum(jnp.where(table, values[None, :] + 1, 0), axis=1) - 1


def shards(sentences, sent_doc, images, image_owner, anchor, loader_shard):
    members = lax.axis_size("docs")
    myself = lax.axis_index("docs")
    own_rows, feature = sentences.shape
    capacity = max(4, 2 * images.shape[0] // members)
    temper = feature ** (-0.5)
    owner_table = slot_table(image_owner[:, 0], members, capacity)
    owner_dispatch = owner_table.astype(jnp.bfloat16)
    extended = extended_2(sentences, (("docs", 0),), MOST_SENT)
    padded_ids = jnp.pad(sent_doc, (MOST_SENT, MOST_SENT), constant_values=-1)
    window_ids = lax.dynamic_slice_in_dim(padded_ids, myself * own_rows, own_rows + 2 * MOST_SENT)
    outgoing = jnp.dot(owner_dispatch, images, preferred_element_type=jnp.float32).astype(
        jnp.bfloat16
    )
    outgoing = outgoing.reshape(members, capacity, feature)
    anchor_slots = spread_values(owner_table, anchor).reshape(members, capacity)
    shard_slots = spread_values(owner_table, loader_shard[:, 0]).reshape(members, capacity)
    out_rows = myself * capacity + ranks_of(loader_shard[:, 0], members)
    row_slots = spread_values(owner_table, out_rows).reshape(members, capacity)
    arrived = lax.all_to_all(outgoing, "docs", split_axis=0, concat_axis=0, tiled=True)
    positions = lax.all_to_all(anchor_slots, "docs", split_axis=0, concat_axis=0, tiled=True)
    shards_in = lax.all_to_all(shard_slots, "docs", split_axis=0, concat_axis=0, tiled=True)
    rows_in = lax.all_to_all(row_slots, "docs", split_axis=0, concat_axis=0, tiled=True)
    items = arrived.shape[1]
    queries = arrived.reshape(members * items, feature)
    spots = positions.reshape(members * items)
    filled = spots >= 0
    docs_of = jnp.where(filled, sent_doc[myself * own_rows + jnp.maximum(spots, 0)], -2)
    scores = (
        lax.dot_general(
            queries, extended, (((1,), (1,)), ((), ())), preferred_element_type=jnp.float32
        )
        * temper
    )
    member = docs_of[:, None] == window_ids[None, :]
    peak = jnp.max(jnp.where(member, scores, -1e30), axis=1, keepdims=True)
    raised = jnp.where(member, jnp.exp(scores - peak), 0.0)
    denominator = jnp.sum(raised, axis=1, keepdims=True)
    weights = (raised / jnp.where(filled[:, None], denominator, 1.0)).astype(jnp.bfloat16)
    aligned = jnp.dot(weights, extended, preferred_element_type=jnp.float32).astype(jnp.bfloat16)
    aligned = aligned.reshape(members, items, feature)
    labels = jnp.arange(members, dtype=jnp.int32)
    route_mask = shards_in[:, None, :] == labels[None, :, None]
    route_weights = route_mask.astype(jnp.bfloat16)
    image_fwd = jnp.einsum(
        "sdj,sje->dje", route_weights, arrived, preferred_element_type=jnp.float32
    ).astype(jnp.bfloat16)
    text_fwd = jnp.einsum(
        "sdj,sje->dje", route_weights, aligned, preferred_element_type=jnp.float32
    ).astype(jnp.bfloat16)
    rows_fwd = (jnp.sum(jnp.where(route_mask, rows_in[:, None, :] + 1, 0), axis=0) - 1).astype(
        jnp.int32
    )
    got_images = lax.all_to_all(image_fwd, "docs", split_axis=0, concat_axis=0, tiled=True)
    got_text = lax.all_to_all(text_fwd, "docs", split_axis=0, concat_axis=0, tiled=True)
    got_rows = lax.all_to_all(rows_fwd, "docs", split_axis=0, concat_axis=0, tiled=True)
    flat_rows = got_rows.reshape(members * capacity)
    block_ids = jnp.arange(members * capacity, dtype=jnp.int32)
    placing = (block_ids[:, None] == flat_rows[None, :]).astype(jnp.bfloat16)
    loaded_images = jnp.dot(
        placing, got_images.reshape(members * capacity, feature), preferred_element_type=jnp.float32
    ).astype(jnp.bfloat16)
    loaded_text = jnp.dot(
        placing, got_text.reshape(members * capacity, feature), preferred_element_type=jnp.float32
    ).astype(jnp.bfloat16)
    return (loaded_images, loaded_text)


def solution(mesh):
    return jax.shard_map(
        shards,
        mesh=mesh,
        in_specs=(
            P(("groups", "docs"), None),
            P("groups"),
            P(("groups", "docs"), None),
            P(("groups", "docs"), None),
            P(("groups", "docs")),
            P(("groups", "docs"), None),
        ),
        out_specs=(P(("groups", "docs"), None), P(("groups", "docs"), None)),
        check_vma=False,
    )
```

profile of v0, /device:TPU:1, one launch (start us, length us, event | category | flops | bytes accessed | tf_op | source)
XLA Modules:
  0.0 170.4 jit_solution(14369713423408936356)
XLA Ops:
  0.7 0.8 fusion.19
  2.2 0.8 fusion.18
  5.2 0.7 broadcast_add_fusion.5
  5.8 0.8 fusion.16
  8.3 7.3 %all-to-all-start.5 = ((s32[16,1,32]{2,1,0:T(1,128)}), s32[16,1,32]{2,1,0:T(1,128)S(1)}, u32[]{:S(2)}, u32[]{:S(2)}) async-start(s32[16,1,32]{2,1,0:T(1,128)} %sub.56), calls=%async_computation.5 | async-start | bytes 16384 | tf_op jit(solution)/shard_map/all_to_all | solution.py:58
  15.7 0.9 fusion.22
  16.6 3.5 %collective-permute-start = (bf16[32,1280]{1,0:T(8,128)(2,1)S(1)}, bf16[32,1280]{1,0:T(8,128)(2,1)S(1)}, u32[]{:S(2)}, u32[]{:S(2)}) collective-permute-start(bf16[32,1280]{1,0:T(8,128)(2,1)S(1)} %get-tuple-element.6), channel_id=1, source_target_pairs={{0,1},{1,2},{2,3},{3,4},{4,5},{5,6},{6,7},{7,8},{8,9},{9,10},{10,1... | collective-permute-start | bytes 245768 | tf_op jit(solution)/shard_map/ppermute | solution.py:16
  20.1 1.9 %collective-permute-start.1 = (bf16[32,1280]{1,0:T(8,128)(2,1)S(1)}, bf16[32,1280]{1,0:T(8,128)(2,1)S(1)}, u32[]{:S(2)}, u32[]{:S(2)}) collective-permute-start(bf16[32,1280]{1,0:T(8,128)(2,1)S(1)} %get-tuple-element.5), channel_id=1, source_target_pairs={{1,0},{2,1},{3,2},{4,3},{5,4},{6,5},{7,6},{8,7},{9,8},{10,9},{11,1... | collective-permute-start | bytes 245768 | tf_op jit(solution)/shard_map/ppermute | solution.py:17
  22.8 6.1 %all-to-all-start = ((s32[16,1,32]{2,1,0:T(1,128)}), s32[16,1,32]{2,1,0:T(1,128)S(1)}, u32[]{:S(2)}, u32[]{:S(2)}) async-start(s32[16,1,32]{2,1,0:T(1,128)} %bitcast.4), calls=%async_computation | async-start | bytes 16384 | tf_op jit(solution)/shard_map/all_to_all | solution.py:59
  28.9 1.6 convolution_convert_fusion.5
  31.1 3.5 %all-to-all-done = s32[16,1,32]{2,1,0:T(1,128)S(1)} async-done(((s32[16,1,32]{2,1,0:T(1,128)}), s32[16,1,32]{2,1,0:T(1,128)S(1)}, u32[]{:S(2)}, u32[]{:S(2)}) %all-to-all-start) | async-done | bytes 2080 | tf_op jit(solution)/shard_map/all_to_all | solution.py:59
  34.6 4.0 %all-to-all-start.1 = ((s32[16,1,32]{2,1,0:T(1,128)}), s32[16,1,32]{2,1,0:T(1,128)S(1)}, u32[]{:S(2)}, u32[]{:S(2)}) async-start(s32[16,1,32]{2,1,0:T(1,128)} %bitcast.8), calls=%async_computation.1 | async-start | bytes 16384 | tf_op jit(solution)/shard_map/all_to_all | solution.py:60
  38.6 0.8 pad_dynamic-slice_fusion
  39.4 5.1 %all-to-all-done.1 = s32[16,1,32]{2,1,0:T(1,128)S(1)} async-done(((s32[16,1,32]{2,1,0:T(1,128)}), s32[16,1,32]{2,1,0:T(1,128)S(1)}, u32[]{:S(2)}, u32[]{:S(2)}) %all-to-all-start.1) | async-done | bytes 2080 | tf_op jit(solution)/shard_map/all_to_all | solution.py:60
  44.5 4.2 %all-to-all-start.3 = ((bf16[16,32,1280]{2,1,0:T(8,128)(2,1)}), bf16[16,32,1280]{2,1,0:T(8,128)(2,1)S(1)}, u32[]{:S(2)}, u32[]{:S(2)}) async-start(bf16[16,32,1280]{2,1,0:T(8,128)(2,1)} %bitcast.11), calls=%async_computation.3 | async-start | bytes 2621440 | tf_op jit(solution)/shard_map/all_to_all | solution.py:57
  48.9 3.1 %gather_fusion = s32[512]{0:T(512)S(1)} fusion(s32[32768]{0:T(1024)S(1)} %copy-done.1, s32[1024]{0:T(1024)S(1)} %pad_clamp_fusion), kind=kCustom, calls=%fused_computation | custom fusion | bytes 6144 | tf_op jit(solution)/shard_map/gather | solution.py:65
  54.3 5.1 %constant_dynamic-update-slice_fusion.1 = bf16[2112,1280]{1,0:T(8,128)(2,1)} fusion(bf16[2112,1280]{1,0:T(8,128)(2,1)} %constant_dynamic-update-slice_fusion.2, bf16[2048,1280]{1,0:T(8,128)(2,1)} %param.6), kind=kLoop, calls=%fused_computation.55 | loop fusion | bytes 10485760
  60.0 16.6 %all-to-all-done.3 = bf16[16,32,1280]{2,1,0:T(8,128)(2,1)S(1)} async-done(((bf16[16,32,1280]{2,1,0:T(8,128)(2,1)}), bf16[16,32,1280]{2,1,0:T(8,128)(2,1)S(1)}, u32[]{:S(2)}, u32[]{:S(2)}) %all-to-all-start.3) | async-done | bytes 1310752 | tf_op jit(solution)/shard_map/all_to_all | solution.py:57
  76.6 7.4 %all-to-all-start.2 = ((s32[16,1,32]{2,1,0:T(1,128)}), s32[16,1,32]{2,1,0:T(1,128)S(1)}, u32[]{:S(2)}, u32[]{:S(2)}) async-start(s32[16,1,32]{2,1,0:T(1,128)} %copy.36), calls=%async_computation.2 | async-start | bytes 16384 | tf_op jit(solution)/shard_map/all_to_all | solution.py:93
  84.1 5.4 %fusion = (f32[512]{0:T(512)S(1)}, f32[512,2112]{0,1:T(8,128)S(1)}) fusion(s32[512]{0:T(512)S(1)} %broadcast_select_fusion.1, s32[2112]{0:T(1024)S(1)} %pad_dynamic-slice_fusion, bf16[512,1280]{1,0:T(8,128)(2,1)S(1)} %bitcast.56, bf16[2112,1280]{1,0:T(8,128)(2,1)} %constant_dynamic-update-slice_fusion), kind=kOutput, calls=%fused_computation.4 | convolution fusion | flops 2772565504 | bytes 11055360 | tf_op jit(solution)/shard_map/dot_general | solution.py:67
  89.5 1.3 fusion.1
  90.8 6.1 %convolution_convert_fusion.2 = bf16[512,1280]{1,0:T(8,128)(2,1)S(1)} fusion(bf16[2112,1280]{1,0:T(8,128)(2,1)} %constant_dynamic-update-slice_fusion, f32[512,2112]{0,1:T(8,128)S(1)} %get-tuple-element.8, f32[512]{0:T(512)S(1)} %broadcast_select_fusion, f32[512]{0:T(512)S(1)} %get-tuple-element.7, s32[512]{0:T(512)S(1)} %broadcast_select_fusion.1, ...), kind=kOutput, calls=%fused_computation.9 | convolution fusion | flops 2774302720 | bytes 11057408 | tf_op jit(solution)/shard_map/dot_general | solution.py:77
  96.9 0.9 fusion.3
  97.9 1.4 copy.40
  99.3 6.0 %all-to-all-start.6 = ((bf16[16,32,1280]{2,1,0:T(8,128)(2,1)}), bf16[16,32,1280]{2,1,0:T(8,128)(2,1)S(1)}, u32[]{:S(2)}, u32[]{:S(2)}) async-start(bf16[16,32,1280]{2,1,0:T(8,128)(2,1)} %copy.40), calls=%async_computation.6 | async-start | bytes 2621440 | tf_op jit(solution)/shard_map/all_to_all | solution.py:92
  105.3 0.9 fusion.2
  106.3 1.4 copy.38
  107.7 25.5 %all-to-all-done.6 = bf16[16,32,1280]{2,1,0:T(8,128)(2,1)S(1)} async-done(((bf16[16,32,1280]{2,1,0:T(8,128)(2,1)}), bf16[16,32,1280]{2,1,0:T(8,128)(2,1)S(1)}, u32[]{:S(2)}, u32[]{:S(2)}) %all-to-all-start.6) | async-done | bytes 1310752 | tf_op jit(solution)/shard_map/all_to_all | solution.py:92
  133.2 7.5 %all-to-all-start.4 = ((bf16[16,32,1280]{2,1,0:T(8,128)(2,1)}), bf16[16,32,1280]{2,1,0:T(8,128)(2,1)S(1)}, u32[]{:S(2)}, u32[]{:S(2)}) async-start(bf16[16,32,1280]{2,1,0:T(8,128)(2,1)} %copy.38), calls=%async_computation.4 | async-start | bytes 2621440 | tf_op jit(solution)/shard_map/all_to_all | solution.py:91
  141.9 1.9 %convolution_convert_fusion = bf16[512,1280]{1,0:T(8,128)(2,1)} fusion(bf16[512,1280]{1,0:T(8,128)(2,1)S(1)} %bitcast.58, s32[512]{0:T(512)S(1)} %eq.124), kind=kOutput, calls=%fused_computation.7 | convolution fusion | flops 672006144 | bytes 2623488 | tf_op jit(solution)/shard_map/dot_general | solution.py:100
  143.8 24.7 %all-to-all-done.4 = bf16[16,32,1280]{2,1,0:T(8,128)(2,1)S(1)} async-done(((bf16[16,32,1280]{2,1,0:T(8,128)(2,1)}), bf16[16,32,1280]{2,1,0:T(8,128)(2,1)S(1)}, u32[]{:S(2)}, u32[]{:S(2)}) %all-to-all-start.4) | async-done | bytes 1310752 | tf_op jit(solution)/shard_map/all_to_all | solution.py:91
  168.5 1.9 %convolution_convert_fusion.3 = bf16[512,1280]{1,0:T(8,128)(2,1)} fusion(bf16[512,1280]{1,0:T(8,128)(2,1)S(1)} %bitcast.59, s32[512]{0:T(512)S(1)} %eq.124), kind=kOutput, calls=%fused_computation.10 | convolution fusion | flops 672006144 | bytes 2623488 | tf_op jit(solution)/shard_map/dot_general | solution.py:97
  (45 shorter events, 10.3 us)
Async XLA Ops:
  0.6 28.3 %copy-start = (bf16[256,1280]{1,0:T(8,128)(2,1)S(1)}, bf16[256,1280]{1,0:T(8,128)(2,1)}, u32[]{:S(2)}) copy-start(bf16[256,1280]{1,0:T(8,128)(2,1)} %param.8) | copy-start | bytes 1966084
  0.6 48.2 %copy-start.1 = (s32[32768]{0:T(1024)S(1)}, s32[32768]{0:T(1024)}, u32[]{:S(2)}) copy-start(s32[32768]{0:T(1024)} %param.7) | copy-start | bytes 393220
  8.3 14.4 %all-to-all-start.5 = ((s32[16,1,32]{2,1,0:T(1,128)}), s32[16,1,32]{2,1,0:T(1,128)S(1)}, u32[]{:S(2)}, u32[]{:S(2)}) async-start(s32[16,1,32]{2,1,0:T(1,128)} %sub.56), calls=%async_computation.5 | async-start | bytes 16384 | tf_op jit(solution)/shard_map/all_to_all | solution.py:58
  16.6 37.0 %collective-permute-start = (bf16[32,1280]{1,0:T(8,128)(2,1)S(1)}, bf16[32,1280]{1,0:T(8,128)(2,1)S(1)}, u32[]{:S(2)}, u32[]{:S(2)}) collective-permute-start(bf16[32,1280]{1,0:T(8,128)(2,1)S(1)} %get-tuple-element.6), channel_id=1, source_target_pairs={{0,1},{1,2},{2,3},{3,4},{4,5},{5,6},{6,7},{7,8},{8,9},{9,10},{10,1... | collective-permute-start | bytes 245768 | tf_op jit(solution)/shard_map/ppermute | solution.py:16
  20.1 39.2 %collective-permute-start.1 = (bf16[32,1280]{1,0:T(8,128)(2,1)S(1)}, bf16[32,1280]{1,0:T(8,128)(2,1)S(1)}, u32[]{:S(2)}, u32[]{:S(2)}) collective-permute-start(bf16[32,1280]{1,0:T(8,128)(2,1)S(1)} %get-tuple-element.5), channel_id=1, source_target_pairs={{1,0},{2,1},{3,2},{4,3},{5,4},{6,5},{7,6},{8,7},{9,8},{10,9},{11,1... | collective-permute-start | bytes 245768 | tf_op jit(solution)/shard_map/ppermute | solution.py:17
  22.8 11.9 %all-to-all-start = ((s32[16,1,32]{2,1,0:T(1,128)}), s32[16,1,32]{2,1,0:T(1,128)S(1)}, u32[]{:S(2)}, u32[]{:S(2)}) async-start(s32[16,1,32]{2,1,0:T(1,128)} %bitcast.4), calls=%async_computation | async-start | bytes 16384 | tf_op jit(solution)/shard_map/all_to_all | solution.py:59
  34.6 9.9 %all-to-all-start.1 = ((s32[16,1,32]{2,1,0:T(1,128)}), s32[16,1,32]{2,1,0:T(1,128)S(1)}, u32[]{:S(2)}, u32[]{:S(2)}) async-start(s32[16,1,32]{2,1,0:T(1,128)} %bitcast.8), calls=%async_computation.1 | async-start | bytes 16384 | tf_op jit(solution)/shard_map/all_to_all | solution.py:60
  44.5 32.1 %all-to-all-start.3 = ((bf16[16,32,1280]{2,1,0:T(8,128)(2,1)}), bf16[16,32,1280]{2,1,0:T(8,128)(2,1)S(1)}, u32[]{:S(2)}, u32[]{:S(2)}) async-start(bf16[16,32,1280]{2,1,0:T(8,128)(2,1)} %bitcast.11), calls=%async_computation.3 | async-start | bytes 2621440 | tf_op jit(solution)/shard_map/all_to_all | solution.py:57
  76.6 22.7 %all-to-all-start.2 = ((s32[16,1,32]{2,1,0:T(1,128)}), s32[16,1,32]{2,1,0:T(1,128)S(1)}, u32[]{:S(2)}, u32[]{:S(2)}) async-start(s32[16,1,32]{2,1,0:T(1,128)} %copy.36), calls=%async_computation.2 | async-start | bytes 16384 | tf_op jit(solution)/shard_map/all_to_all | solution.py:93
  99.3 33.9 %all-to-all-start.6 = ((bf16[16,32,1280]{2,1,0:T(8,128)(2,1)}), bf16[16,32,1280]{2,1,0:T(8,128)(2,1)S(1)}, u32[]{:S(2)}, u32[]{:S(2)}) async-start(bf16[16,32,1280]{2,1,0:T(8,128)(2,1)} %copy.40), calls=%async_computation.6 | async-start | bytes 2621440 | tf_op jit(solution)/shard_map/all_to_all | solution.py:92
  133.2 35.3 %all-to-all-start.4 = ((bf16[16,32,1280]{2,1,0:T(8,128)(2,1)}), bf16[16,32,1280]{2,1,0:T(8,128)(2,1)S(1)}, u32[]{:S(2)}, u32[]{:S(2)}) async-start(bf16[16,32,1280]{2,1,0:T(8,128)(2,1)} %copy.38), calls=%async_computation.4 | async-start | bytes 2621440 | tf_op jit(solution)/shard_map/all_to_all | solution.py:91
where the time goes:
time: 173 us; the launch traced here: 170 us
  waiting for transfers between devices  75.3 us (44%)
  starting transfers between devices  48.1 us (28%)
  matrix products  18.8 us (11%)
  local copies, waits for them, and re-layouts  18.1 us (10%)
  other arithmetic  9.28 us (5%)
    all_to_all x1, waiting for transfers between devices, shards(): lax.all_to_all(text_fwd, 'docs', split_axis=0, concat_axis=0, tiled=True)  25.5 us
    all_to_all x1, waiting for transfers between devices, shards(): lax.all_to_all(image_fwd, 'docs', split_axis=0, concat_axis=0, tiled=True)  24.7 us
    all_to_all x1, waiting for transfers between devices, shards(): lax.all_to_all(outgoing, 'docs', split_axis=0, concat_axis=0, tiled=True)  16.6 us
    all_to_all x1, starting transfers between devices, shards(): lax.all_to_all(image_fwd, 'docs', split_axis=0, concat_axis=0, tiled=True)  7.46 us
    all_to_all x1, starting transfers between devices, shards(): lax.all_to_all(rows_fwd, 'docs', split_axis=0, concat_axis=0, tiled=True)  7.44 us
    all_to_all x1, starting transfers between devices, shards(): lax.all_to_all(anchor_slots, 'docs', split_axis=0, concat_axis=0, tiled=T...  7.34 us
    all_to_all x1, starting transfers between devices, shards(): lax.all_to_all(shard_slots, 'docs', split_axis=0, concat_axis=0, tiled=True)  6.12 us
    dot_general x1, matrix products, shards(): jnp.dot(weights, extended, preferred_element_type=jnp.float32)  6.08 us
  transfers between devices with their start and end apart: 9, of which 5 were waited for; matrix products, arithmetic and copies ran while one was open for 21% of the time, Pallas kernels for 0%

commit v1 on v0

v1 whole, which is shorter than its diff:
```python
import functools

import jax
import jax.numpy as jnp
from jax import lax
from jax.experimental import pallas as pl
from jax.experimental.pallas import tpu as pltpu
from jax.sharding import PartitionSpec as P

MOST_SENT = 32
LANES = 128
SUB = 8
MESH = pl.DeviceIdType.MESH
HIGH = lax.Precision.HIGHEST
TRANS_LHS = (((0,), (0,)), ((), ()))
TRANS_RHS = (((1,), (1,)), ((), ()))


def iota(shape, dim):
    return lax.broadcasted_iota(jnp.int32, shape, dim)


def exchange_kernel(
    n, cap, block, tile, cols_ref, images_ref, ids_ref, sent_ref,
    img_out, txt_out, meta_out,
    ext, disp, shrd, arrived, aligned, tsend, meta_s, target_ref,
    local_sem, halo_send, halo_recv, send_sem, recv_sem,
):
    me = lax.axis_index("docs")
    own_rows, feature = sent_ref.shape
    width = ext.shape[0]
    count = images_ref.shape[0]
    rows = n * block
    temper = feature ** (-0.5)

    barrier = pltpu.get_barrier_semaphore()

    @pl.loop(1, n)
    def _(k):
        pl.semaphore_signal(barrier, inc=1, device_id={"docs": lax.rem(me + k, n)}, device_id_type=MESH)

    load = pltpu.make_async_copy(sent_ref, ext.at[pl.ds(MOST_SENT, own_rows)], local_sem.at[0])
    load.start()

    owner, anchor, shard = cols_ref[:, 0:1], cols_ref[:, 1:2], cols_ref[:, 2:3]
    wide = max(LANES, n)
    onehot = (owner == iota((count, wide), 1)).astype(jnp.float32)
    below = (iota((count, count), 0) > iota((count, count), 1)).astype(jnp.bfloat16)
    counts = jnp.dot(below, onehot.astype(jnp.bfloat16), preferred_element_type=jnp.float32)
    rank = jnp.sum(counts * onehot, axis=1, keepdims=True).astype(jnp.int32)
    lane = iota((count, LANES), 1)
    first = rank == 0
    for_owner = jnp.where(lane == rank, anchor + 1, 0) + jnp.where((lane == cap) & first, shard + 1, 0)
    for_shard = jnp.where((lane == cap + 1) & first, owner + 1, 0)
    keyed = iota((count, n * SUB), 1)
    meta = lax.dot_general(
        (keyed == owner * SUB).astype(jnp.float32), for_owner.astype(jnp.float32), TRANS_LHS,
        precision=HIGH, preferred_element_type=jnp.float32,
    ) + lax.dot_general(
        (keyed == shard * SUB).astype(jnp.float32), for_shard.astype(jnp.float32), TRANS_LHS,
        precision=HIGH, preferred_element_type=jnp.float32,
    )
    meta_s[...] = meta.astype(jnp.int32)

    def fill(ref, key):
        place = key * block + rank

        @pl.loop(0, rows // tile)
        def _(t):
            base = pl.multiple_of(t * tile, tile)
            table = (place == iota((count, tile), 1) + base).astype(jnp.bfloat16)
            ref[pl.ds(base, tile), :] = lax.dot_general(
                table, images_ref[...], TRANS_LHS, preferred_element_type=jnp.float32
            ).astype(jnp.bfloat16)

    fill(disp, owner)
    fill(shrd, shard)
    pl.semaphore_wait(barrier, n - 1)

    def at(ref, who, size):
        return ref.at[pl.ds(pl.multiple_of(who * size, size), size)]

    def remote(kind, src, dst, size, peer, slot):
        return pltpu.make_async_remote_copy(
            src_ref=at(src, peer, size), dst_ref=at(dst, slot, size),
            send_sem=send_sem.at[kind, peer], recv_sem=recv_sem.at[kind, slot],
            device_id={"docs": peer}, device_id_type=MESH,
        )

    flows = ((meta_s, meta_out, SUB), (disp, arrived, block), (shrd, img_out, block), (tsend, txt_out, block))

    def start(kind):
        src, dst, size = flows[kind]

        @pl.loop(1, n)
        def _(k):
            remote(kind, src, dst, size, lax.rem(me + k, n), me).start()

        pltpu.make_async_copy(at(src, me, size), at(dst, me, size), local_sem.at[1 + kind]).start()

    def finish(kind, sent):
        src, dst, size = flows[kind]

        @pl.loop(1, n)
        def _(k):
            peer = lax.rem(me + k, n)
            if sent:
                remote(kind, src, dst, size, peer, me).wait_send()
            else:
                remote(kind, src, dst, size, peer, peer).wait_recv()

        if not sent:
            pltpu.make_async_copy(at(src, me, size), at(dst, me, size), local_sem.at[1 + kind]).wait()

    def halo(way):
        to = lax.rem(me + 1, n) if way == 0 else lax.rem(me + n - 1, n)
        src = own_rows - MOST_SENT if way == 0 else 0
        dst = 0 if way == 0 else own_rows + MOST_SENT
        return pltpu.make_async_remote_copy(
            src_ref=sent_ref.at[pl.ds(src, MOST_SENT)], dst_ref=ext.at[pl.ds(dst, MOST_SENT)],
            send_sem=halo_send.at[way], recv_sem=halo_recv.at[way],
            device_id={"docs": to}, device_id_type=MESH,
        )

    start(0)
    halo(0).start()
    halo(1).start()
    start(1)
    start(2)
    load.wait()
    for way in (0, 1):
        halo(way).wait_recv()
    finish(0, False)
    finish(1, False)

    ids = ids_ref[...]
    records = meta_out[...].astype(jnp.float32)

    @pl.loop(0, rows // tile)
    def _(t):
        base = pl.multiple_of(t * tile, tile)
        spot = iota((tile, n * SUB), 0) + base
        picker = (lax.div(spot, block) * SUB == iota((tile, n * SUB), 1)).astype(jnp.float32)
        picked = jnp.dot(picker, records, precision=HIGH, preferred_element_type=jnp.float32)
        picked = picked.astype(jnp.int32)
        step = lax.rem(iota((tile, 1), 0) + base, block)
        lanes = iota((tile, LANES), 1)
        anchored = jnp.sum(jnp.where((lanes == step) & (lanes < cap), picked, 0), axis=1, keepdims=True)
        goal = jnp.sum(jnp.where(lanes == cap, picked, 0), axis=1, keepdims=True)
        target_ref[pl.ds(base, tile), :] = (goal - 1) * block + step
        filled = anchored > 0
        here = iota((tile, width), 1) == anchored - 1 + MOST_SENT
        doc = jnp.sum(jnp.where(here, ids, 0), axis=1, keepdims=True)
        doc = jnp.where(filled, doc, -2)
        scores = lax.dot_general(
            arrived[pl.ds(base, tile), :], ext[...], TRANS_RHS, preferred_element_type=jnp.float32
        ) * temper
        member = doc == ids
        peak = jnp.max(jnp.where(member, scores, -1e30), axis=1, keepdims=True)
        raised = jnp.where(member, jnp.exp(scores - peak), 0.0)
        total = jnp.sum(raised, axis=1, keepdims=True)
        weights = (raised / jnp.where(filled, total, 1.0)).astype(jnp.bfloat16)
        aligned[pl.ds(base, tile), :] = jnp.dot(
            weights, ext[...], preferred_element_type=jnp.float32
        ).astype(jnp.bfloat16)

    @pl.loop(0, rows // tile)
    def _(t):
        base = pl.multiple_of(t * tile, tile)
        table = (target_ref[...] == iota((rows, tile), 1) + base).astype(jnp.bfloat16)
        tsend[pl.ds(base, tile), :] = lax.dot_general(
            table, aligned[...], TRANS_LHS, preferred_element_type=jnp.float32
        ).astype(jnp.bfloat16)

    start(3)
    for way in (0, 1):
        halo(way).wait_send()
    finish(0, True)
    finish(1, True)
    finish(2, True)
    finish(2, False)
    finish(3, True)
    finish(3, False)


def place_kernel(n, block, lane, meta_ref, img_ref, txt_ref, img_out, txt_out, buf, sems):
    copy = pltpu.make_async_copy(img_ref, img_out, sems.at[0])
    copy.start()
    for s in range(n):
        source = meta_ref[s * SUB, lane]
        rows = txt_ref[pl.ds(pl.multiple_of(jnp.maximum(source - 1, 0) * block, block), block), :]
        buf[pl.ds(s * block, block), :] = jnp.where(source > 0, rows, jnp.zeros_like(rows))
        pltpu.make_async_copy(
            buf.at[pl.ds(s * block, block)], txt_out.at[pl.ds(s * block, block)], sems.at[1 + s]
        ).start()
    for s in range(n):
        pltpu.make_async_copy(
            buf.at[pl.ds(s * block, block)], txt_out.at[pl.ds(s * block, block)], sems.at[1 + s]
        ).wait()
    copy.wait()


def shards(sentences, sent_doc, images, image_owner, anchor, loader_shard):
    n = lax.axis_size("docs")
    me = lax.axis_index("docs")
    own_rows, feature = sentences.shape
    count = images.shape[0]
    cap = max(4, 2 * count // n)
    block = -(-cap // 16) * 16
    rows = n * block
    tile = min(256, rows)
    width = own_rows + 2 * MOST_SENT
    padded_ids = jnp.pad(sent_doc, (MOST_SENT, MOST_SENT), constant_values=-1)
    ids = lax.dynamic_slice_in_dim(padded_ids, me * own_rows, width)[None, :]
    cols = jnp.concatenate([image_owner, anchor[:, None], loader_shard], axis=1)
    half = jax.ShapeDtypeStruct((rows, feature), jnp.bfloat16)
    slots = pltpu.VMEM((rows, feature), jnp.bfloat16)
    dma = pltpu.SemaphoreType.DMA
    vmem = pl.BlockSpec(memory_space=pltpu.VMEM)
    got_img, got_txt, meta = pl.pallas_call(
        functools.partial(exchange_kernel, n, cap, block, tile),
        out_shape=(half, half, jax.ShapeDtypeStruct((n * SUB, LANES), jnp.int32)),
        in_specs=[vmem, vmem, vmem, pl.BlockSpec(memory_space=pl.ANY)],
        out_specs=(vmem, vmem, vmem),
        scratch_shapes=[
            pltpu.VMEM((width, feature), jnp.bfloat16),
            slots, slots, slots, slots, slots,
            pltpu.VMEM((n * SUB, LANES), jnp.int32),
            pltpu.VMEM((rows, 1), jnp.int32),
            dma((5,)), dma((2,)), dma((2,)), dma((4, n)), dma((4, n)),
        ],
        compiler_params=pltpu.CompilerParams(
            collective_id=0, has_side_effects=True, vmem_limit_bytes=60 * 1024 * 1024
        ),
    )(cols, images, ids, sentences)
    if block != cap:
        meta = meta.reshape(n, SUB, LANES)[:, 0, cap + 1]
        picked = got_txt.reshape(n, block, feature)[jnp.maximum(meta - 1, 0), :cap]
        text = jnp.where((meta > 0)[:, None, None], picked, jnp.zeros_like(picked))
        image = got_img.reshape(n, block, feature)[:, :cap]
        return (image.reshape(n * cap, feature), text.reshape(n * cap, feature))
    return pl.pallas_call(
        functools.partial(place_kernel, n, block, cap + 1),
        out_shape=(half, half),
        in_specs=[pl.BlockSpec(memory_space=pltpu.SMEM), vmem, vmem],
        out_specs=(pl.BlockSpec(memory_space=pl.ANY), pl.BlockSpec(memory_space=pl.ANY)),
        scratch_shapes=[slots, dma((1 + n,))],
    )(meta, got_img, got_txt)


def solution(mesh):
    return jax.shard_map(
        shards,
        mesh=mesh,
        in_specs=(
            P(("groups", "docs"), None),
            P("groups"),
            P(("groups", "docs"), None),
            P(("groups", "docs"), None),
            P(("groups", "docs")),
            P(("groups", "docs"), None),
        ),
        out_specs=(P(("groups", "docs"), None), P(("groups", "docs"), None)),
        check_vma=False,
    )
```

time: 173 us -> 103 us (0.60)
  the two profiles are of different devices: /device:TPU:1 before, /device:TPU:13 now
where the time goes in v1:
time: 103 us
  Pallas kernels  99 us (96%)
  local copies, waits for them, and re-layouts  2.21 us (2%)
    pallas_call x1, Pallas kernels, shards(): pl.pallas_call(functools.partial(exchange_kernel, n, cap, block, tile), o...  95.7 us
    pallas_call x1, Pallas kernels, shards(): pl.pallas_call(functools.partial(place_kernel, n, block, cap + 1), out_sh...  3.36 us

profile of v1, /device:TPU:13, one launch (start us, length us, event | category | flops | bytes accessed | tf_op | source)
XLA Modules:
  0.0 102.6 jit_solution(9403102166141082327)
XLA Ops:
  0.6 0.7 pad_add_fusion
  1.4 0.8 pad_dynamic-slice_fusion
  2.2 0.6 broadcast_in_dim.7.ids_ref
  2.8 0.8 copy.13.cols_ref
  3.6 95.7 %shard_map.77 = (bf16[512,1280]{1,0:T(8,128)(2,1)}, bf16[512,1280]{1,0:T(8,128)(2,1)}, s32[128,128]{1,0:T(8,128)}) custom-call(s32[256,3]{1,0:T(8,128)} %copy.13.cols_ref, bf16[256,1280]{1,0:T(8,128)(2,1)} %images_ref.1, s32[1,2112]{1,0:T(1,128)} %broadcast_in_dim.7.ids_ref, bf16[2048,1280]{1,0:T(8,128)(2,1)} %sent_ref.1), custom_call_target="tpu_custom_call" | custom-call | tf_op jit(solution)/shard_map/pallas_call | solution.py:220
  99.3 3.4 %shard_map.78 = (bf16[512,1280]{1,0:T(8,128)(2,1)}, bf16[512,1280]{1,0:T(8,128)(2,1)}) custom-call(s32[128,128]{1,0:T(8,128)} %get-tuple-element.5.meta_ref, bf16[512,1280]{1,0:T(8,128)(2,1)} %get-tuple-element.6.img_ref, bf16[512,1280]{1,0:T(8,128)(2,1)} %get-tuple-element.7.txt_ref), custom_call_target="tpu_custom_call" | custom-call | tf_op jit(solution)/shard_map/pallas_call | solution.py:242

commit v2 on v1

v2 whole, which is shorter than its diff:
```python
import functools

import jax
import jax.numpy as jnp
from jax import lax
from jax.experimental import pallas as pl
from jax.experimental.pallas import tpu as pltpu
from jax.sharding import PartitionSpec as P

MOST_SENT = 32
LANES = 128
SUB = 8
MESH = pl.DeviceIdType.MESH
HIGH = lax.Precision.HIGHEST
TRANS_LHS = (((0,), (0,)), ((), ()))
TRANS_RHS = (((1,), (1,)), ((), ()))


def iota(shape, dim):
    return lax.broadcasted_iota(jnp.int32, shape, dim)


def ranks(keys, n):
    count = keys.shape[1]
    onehot = (keys == iota((n, count), 0)).astype(jnp.float32)
    above = (iota((count, count), 0) < iota((count, count), 1)).astype(jnp.bfloat16)
    counts = jnp.dot(onehot.astype(jnp.bfloat16), above, preferred_element_type=jnp.float32)
    return jnp.sum(counts * onehot, axis=0, keepdims=True).astype(jnp.int32)


def exchange_kernel(
    n, cap, block, tile, rows_ref, images_ref, ids_ref, sent_ref,
    img_out, txt_out, meta_out,
    ext, far_images, far_rows, disp, shrd, far_disp, far_shrd, arrived, aligned, tsend, meta_s, target_ref,
    local_sem, halo_send, halo_recv, raw_send, raw_recv, send_sem, recv_sem,
):
    me = lax.axis_index("docs")
    half = n // 2
    first = lax.div(me, half) * half
    across = lax.rem(first + half, n)
    partner = lax.rem(me + half, n)
    own_rows, feature = sent_ref.shape
    width = ext.shape[0]
    count = images_ref.shape[0]
    rows = n * block
    part = half * block
    temper = feature ** (-0.5)

    barrier = pltpu.get_barrier_semaphore()

    @pl.loop(1, n)
    def _(k):
        pl.semaphore_signal(barrier, inc=1, device_id={"docs": lax.rem(me + k, n)}, device_id_type=MESH)

    load = pltpu.make_async_copy(sent_ref, ext.at[pl.ds(MOST_SENT, own_rows)], local_sem.at[0])
    load.start()
    pl.semaphore_wait(barrier, n - 1)

    def raw(which):
        src, dst = ((rows_ref, far_rows), (images_ref, far_images))[which]
        return pltpu.make_async_remote_copy(
            src_ref=src, dst_ref=dst, send_sem=raw_send.at[which], recv_sem=raw_recv.at[which],
            device_id={"docs": partner}, device_id_type=MESH,
        )

    def halo(way):
        to = lax.rem(me + 1, n) if way == 0 else lax.rem(me + n - 1, n)
        src = own_rows - MOST_SENT if way == 0 else 0
        dst = 0 if way == 0 else own_rows + MOST_SENT
        return pltpu.make_async_remote_copy(
            src_ref=sent_ref.at[pl.ds(src, MOST_SENT)], dst_ref=ext.at[pl.ds(dst, MOST_SENT)],
            send_sem=halo_send.at[way], recv_sem=halo_recv.at[way],
            device_id={"docs": to}, device_id_type=MESH,
        )

    halo(0).start()
    halo(1).start()
    raw(0).start()
    raw(1).start()

    owner, anchor, shard = rows_ref[0:1, :], rows_ref[1:2, :], rows_ref[2:3, :]
    rank = ranks(owner, n)
    lane = iota((LANES, count), 0)
    lead = rank == 0
    for_owner = jnp.where(lane == rank, anchor + 1, 0) + jnp.where((lane == cap) & lead, shard + 1, 0)
    for_shard = jnp.where((lane == cap + 1) & lead, owner + 1, 0)
    keyed = iota((n * SUB, count), 0)
    meta = lax.dot_general(
        (keyed == owner * SUB).astype(jnp.float32), for_owner.astype(jnp.float32), TRANS_RHS,
        precision=HIGH, preferred_element_type=jnp.float32,
    ) + lax.dot_general(
        (keyed == shard * SUB).astype(jnp.float32), for_shard.astype(jnp.float32), TRANS_RHS,
        precision=HIGH, preferred_element_type=jnp.float32,
    )
    meta_s[...] = meta.astype(jnp.int32)

    def fill(ref, key, order, values):
        place = key * block + order

        @pl.loop(0, part // tile)
        def _(t):
            base = pl.multiple_of(t * tile, tile)
            table = (place == iota((tile, count), 0) + (base + first * block)).astype(jnp.bfloat16)
            ref[pl.ds(base, tile), :] = jnp.dot(
                table, values[...], preferred_element_type=jnp.float32
            ).astype(jnp.bfloat16)

    fill(disp, owner, rank, images_ref)
    fill(shrd, shard, rank, images_ref)

    def at(ref, who, size):
        return ref.at[pl.ds(pl.multiple_of(who * size, size), size)]

    flows = (
        (meta_s, meta_out, SUB, True, False),
        (disp, arrived, block, False, False),
        (shrd, img_out, block, False, False),
        (tsend, txt_out, block, True, False),
        (far_disp, arrived, block, False, True),
        (far_shrd, img_out, block, False, True),
    )

    def remote(kind, peer, sender):
        src, dst, size, everyone, far = flows[kind]
        piece = peer if everyone else lax.rem(peer, half)
        slot = lax.rem(sender + half, n) if far else sender
        return pltpu.make_async_remote_copy(
            src_ref=at(src, piece, size), dst_ref=at(dst, slot, size),
            send_sem=send_sem.at[kind, peer], recv_sem=recv_sem.at[kind, sender],
            device_id={"docs": peer}, device_id_type=MESH,
        )

    def local(kind):
        src, dst, size, everyone, far = flows[kind]
        piece = me if everyone else me - first
        slot = partner if far else me
        return pltpu.make_async_copy(at(src, piece, size), at(dst, slot, size), local_sem.at[1 + kind])

    def each(kind, act):
        if flows[kind][3]:

            @pl.loop(0, half)
            def _(k):
                act(across + lax.rem(me - first + k, half))

        @pl.loop(1, half)
        def _(k):
            act(first + lax.rem(me - first + k, half))

    def start(kind):
        each(kind, lambda peer: remote(kind, peer, me).start())
        local(kind).start()

    def sent(kind):
        each(kind, lambda peer: remote(kind, peer, me).wait_send())

    def landed(kind):
        each(kind, lambda peer: remote(kind, peer, peer).wait_recv())
        local(kind).wait()

    start(0)
    start(1)
    start(2)
    load.wait()
    for way in (0, 1):
        halo(way).wait_recv()
    landed(0)
    ids = ids_ref[...]
    records = meta_out[...].astype(jnp.float32)

    def align(head):
        @pl.loop(0, part // tile)
        def _(t):
            base = pl.multiple_of(head * block + t * tile, tile)
            spot = iota((tile, n * SUB), 0) + base
            picker = (lax.div(spot, block) * SUB == iota((tile, n * SUB), 1)).astype(jnp.float32)
            picked = jnp.dot(picker, records, precision=HIGH, preferred_element_type=jnp.float32)
            picked = picked.astype(jnp.int32)
            step = lax.rem(iota((tile, 1), 0) + base, block)
            lanes = iota((tile, LANES), 1)
            anchored = jnp.sum(jnp.where((lanes == step) & (lanes < cap), picked, 0), axis=1, keepdims=True)
            goal = jnp.sum(jnp.where(lanes == cap, picked, 0), axis=1, keepdims=True)
            target_ref[pl.ds(base, tile), :] = (goal - 1) * block + step
            filled = anchored > 0
            here = iota((tile, width), 1) == anchored - 1 + MOST_SENT
            doc = jnp.sum(jnp.where(here, ids, 0), axis=1, keepdims=True)
            doc = jnp.where(filled, doc, -2)
            scores = lax.dot_general(
                arrived[pl.ds(base, tile), :], ext[...], TRANS_RHS, preferred_element_type=jnp.float32
            ) * temper
            member = doc == ids
            peak = jnp.max(jnp.where(member, scores, -1e30), axis=1, keepdims=True)
            raised = jnp.where(member, jnp.exp(scores - peak), 0.0)
            total = jnp.sum(raised, axis=1, keepdims=True)
            weights = (raised / jnp.where(filled, total, 1.0)).astype(jnp.bfloat16)
            aligned[pl.ds(base, tile), :] = jnp.dot(
                weights, ext[...], preferred_element_type=jnp.float32
            ).astype(jnp.bfloat16)

    def route(head, more):
        begin = pl.multiple_of(head * block, part)

        @pl.loop(0, rows // tile)
        def _(t):
            base = pl.multiple_of(t * tile, tile)
            table = target_ref[pl.ds(begin, part), :] == iota((part, tile), 1) + base
            moved = lax.dot_general(
                table.astype(jnp.bfloat16), aligned[pl.ds(begin, part), :], TRANS_LHS,
                preferred_element_type=jnp.float32,
            ).astype(jnp.bfloat16)
            if more:
                moved = tsend[pl.ds(base, tile), :] + moved
            tsend[pl.ds(base, tile), :] = moved

    landed(1)
    align(first)
    route(first, False)
    raw(0).wait_recv()
    far_owner, far_shard = far_rows[0:1, :], far_rows[2:3, :]
    far_rank = ranks(far_owner, n)
    raw(1).wait_recv()
    fill(far_disp, far_owner, far_rank, far_images)
    fill(far_shrd, far_shard, far_rank, far_images)
    start(4)
    start(5)
    landed(4)
    align(across)
    route(across, True)
    start(3)
    for way in (0, 1):
        halo(way).wait_send()
        raw(way).wait_send()
    for kind in (0, 1, 2, 4, 5):
        sent(kind)
    landed(2)
    landed(5)
    sent(3)
    landed(3)


def place_kernel(n, block, lane, meta_ref, img_ref, txt_ref, img_out, txt_out, buf, sems):
    copy = pltpu.make_async_copy(img_ref, img_out, sems.at[0])
    copy.start()
    for s in range(n):
        source = meta_ref[s * SUB, lane]
        rows = txt_ref[pl.ds(pl.multiple_of(jnp.maximum(source - 1, 0) * block, block), block), :]
        buf[pl.ds(s * block, block), :] = jnp.where(source > 0, rows, jnp.zeros_like(rows))
        pltpu.make_async_copy(
            buf.at[pl.ds(s * block, block)], txt_out.at[pl.ds(s * block, block)], sems.at[1 + s]
        ).start()
    for s in range(n):
        pltpu.make_async_copy(
            buf.at[pl.ds(s * block, block)], txt_out.at[pl.ds(s * block, block)], sems.at[1 + s]
        ).wait()
    copy.wait()


def shards(sentences, sent_doc, images, image_owner, anchor, loader_shard):
    n = lax.axis_size("docs")
    me = lax.axis_index("docs")
    own_rows, feature = sentences.shape
    count = images.shape[0]
    cap = max(4, 2 * count // n)
    block = -(-cap // 16) * 16
    rows = n * block
    tile = min(256, rows // 2)
    width = own_rows + 2 * MOST_SENT
    padded_ids = jnp.pad(sent_doc, (MOST_SENT, MOST_SENT), constant_values=-1)
    ids = lax.dynamic_slice_in_dim(padded_ids, me * own_rows, width)[None, :]
    blank = jnp.zeros((SUB - 3, count), jnp.int32)
    table = jnp.concatenate([image_owner.T, anchor[None, :], loader_shard.T, blank], axis=0)
    half = jax.ShapeDtypeStruct((rows, feature), jnp.bfloat16)
    slots = pltpu.VMEM((rows, feature), jnp.bfloat16)
    some = pltpu.VMEM((rows // 2, feature), jnp.bfloat16)
    anywhere = pl.BlockSpec(memory_space=pl.ANY)
    dma = pltpu.SemaphoreType.DMA
    vmem = pl.BlockSpec(memory_space=pltpu.VMEM)
    got_img, got_txt, meta = pl.pallas_call(
        functools.partial(exchange_kernel, n, cap, block, tile),
        out_shape=(half, half, jax.ShapeDtypeStruct((n * SUB, LANES), jnp.int32)),
        in_specs=[vmem, vmem, vmem, anywhere],
        out_specs=(anywhere, anywhere, vmem),
        scratch_shapes=[
            pltpu.VMEM((width, feature), jnp.bfloat16),
            pltpu.VMEM((count, feature), jnp.bfloat16),
            pltpu.VMEM((SUB, count), jnp.int32),
            some, some, some, some, slots, slots, slots,
            pltpu.VMEM((n * SUB, LANES), jnp.int32),
            pltpu.VMEM((rows, 1), jnp.int32),
            dma((7,)), dma((2,)), dma((2,)), dma((2,)), dma((2,)), dma((6, n)), dma((6, n)),
        ],
        compiler_params=pltpu.CompilerParams(
            collective_id=0, has_side_effects=True, vmem_limit_bytes=60 * 1024 * 1024
        ),
    )(table, images, ids, sentences)
    if block != cap:
        meta = meta.reshape(n, SUB, LANES)[:, 0, cap + 1]
        picked = got_txt.reshape(n, block, feature)[jnp.maximum(meta - 1, 0), :cap]
        text = jnp.where((meta > 0)[:, None, None], picked, jnp.zeros_like(picked))
        image = got_img.reshape(n, block, feature)[:, :cap]
        return (image.reshape(n * cap, feature), text.reshape(n * cap, feature))
    return pl.pallas_call(
        functools.partial(place_kernel, n, block, cap + 1),
        out_shape=(half, half),
        in_specs=[pl.BlockSpec(memory_space=pltpu.SMEM), vmem, vmem],
        out_specs=(anywhere, anywhere),
        scratch_shapes=[slots, dma((1 + n,))],
    )(meta, got_img, got_txt)


def solution(mesh):
    return jax.shard_map(
        shards,
        mesh=mesh,
        in_specs=(
            P(("groups", "docs"), None),
            P("groups"),
            P(("groups", "docs"), None),
            P(("groups", "docs"), None),
            P(("groups", "docs")),
            P(("groups", "docs"), None),
        ),
        out_specs=(P(("groups", "docs"), None), P(("groups", "docs"), None)),
        check_vma=False,
    )
```

time: 103 us -> 102 us (level)
  the two profiles are of different devices: /device:TPU:13 before, /device:TPU:1 now
where the time goes in v2:
time: 102 us; the launch traced here: 101 us
  Pallas kernels  97.9 us (96%)
  local copies, waits for them, and re-layouts  1.48 us (1%)
  other arithmetic  1.38 us (1%)
    pallas_call x1, Pallas kernels, shards(): pl.pallas_call(functools.partial(exchange_kernel, n, cap, block, tile), o...  94.6 us
    pallas_call x1, Pallas kernels, shards(): pl.pallas_call(functools.partial(place_kernel, n, block, cap + 1), out_sh...  3.36 us

profile of v2, /device:TPU:1, one launch (start us, length us, event | category | flops | bytes accessed | tf_op | source)
XLA Modules:
  0.0 101.4 jit_solution(7334581444539824577)
XLA Ops:
  0.6 0.1 pad.8.clone
  0.7 1.4 %add_add_fusion.rows_ref = s32[8,256]{1,0:T(8,128)} fusion(s32[1,256]{1,0:T(1,128)} %bitcast.3, s32[1,256]{1,0:T(1,128)} %bitcast.4, s32[1,256]{1,0:T(1,128)} %bitcast.5, s32[8]{0:T(128)S(1)} %pad.8.clone), kind=kLoop, calls=%fused_computation.1 | loop fusion | flops 6144 | bytes 11296 | tf_op jit(solution)/shard_map/concatenate | solution.py:271
  2.1 0.8 pad_dynamic-slice_fusion
  2.9 0.6 broadcast_in_dim.11.ids_ref
  3.5 94.6 %shard_map.77 = (bf16[512,1280]{1,0:T(8,128)(2,1)}, bf16[512,1280]{1,0:T(8,128)(2,1)}, s32[128,128]{1,0:T(8,128)}) custom-call(s32[8,256]{1,0:T(8,128)} %add_add_fusion.rows_ref, bf16[256,1280]{1,0:T(8,128)(2,1)} %images_ref.1, s32[1,2112]{1,0:T(1,128)} %broadcast_in_dim.11.ids_ref, bf16[2048,1280]{1,0:T(8,128)(2,1)} %sent_ref.1), custom_call_target="tpu_custom_call" | custom-call | tf_op jit(solution)/shard_map/pallas_call | solution.py:278
  98.1 3.4 %shard_map.78 = (bf16[512,1280]{1,0:T(8,128)(2,1)}, bf16[512,1280]{1,0:T(8,128)(2,1)}) custom-call(s32[128,128]{1,0:T(8,128)} %get-tuple-element.5.meta_ref, bf16[512,1280]{1,0:T(8,128)(2,1)} %get-tuple-element.6.img_ref, bf16[512,1280]{1,0:T(8,128)(2,1)} %get-tuple-element.7.txt_ref), custom_call_target="tpu_custom_call" | custom-call | tf_op jit(solution)/shard_map/pallas_call | solution.py:302
  (1 shorter events, 0.0 us)

commit v3 on v2

--- a/solution.py
+++ b/solution.py
@@ -29,9 +29,9 @@
 
 
 def exchange_kernel(
-    n, cap, block, tile, rows_ref, images_ref, ids_ref, sent_ref,
+    n, cap, block, tile, owner_ref, anchor_ref, shard_ref, images_ref, ids_ref, sent_ref,
     img_out, txt_out, meta_out,
-    ext, far_images, far_rows, disp, shrd, far_disp, far_shrd, arrived, aligned, tsend, meta_s, target_ref,
+    ext, far_images, far_owner_ref, far_shard_ref, disp, shrd, far_disp, far_shrd, arrived, aligned, tsend, meta_s, target_ref,
     local_sem, halo_send, halo_recv, raw_send, raw_recv, send_sem, recv_sem,
 ):
     me = lax.axis_index("docs")
@@ -57,7 +57,7 @@
     pl.semaphore_wait(barrier, n - 1)
 
     def raw(which):
-        src, dst = ((rows_ref, far_rows), (images_ref, far_images))[which]
+        src, dst = ((owner_ref, far_owner_ref), (shard_ref, far_shard_ref), (images_ref, far_images))[which]
         return pltpu.make_async_remote_copy(
             src_ref=src, dst_ref=dst, send_sem=raw_send.at[which], recv_sem=raw_recv.at[which],
             device_id={"docs": partner}, device_id_type=MESH,
@@ -75,10 +75,10 @@
 
     halo(0).start()
     halo(1).start()
-    raw(0).start()
-    raw(1).start()
-
-    owner, anchor, shard = rows_ref[0:1, :], rows_ref[1:2, :], rows_ref[2:3, :]
+    for which in range(3):
+        raw(which).start()
+
+    owner, anchor, shard = owner_ref[...], anchor_ref[...], shard_ref[...]
     rank = ranks(owner, n)
     lane = iota((LANES, count), 0)
     lead = rank == 0
@@ -216,21 +216,24 @@
     align(first)
     route(first, False)
     raw(0).wait_recv()
-    far_owner, far_shard = far_rows[0:1, :], far_rows[2:3, :]
+    raw(1).wait_recv()
+    far_owner, far_shard = far_owner_ref[...], far_shard_ref[...]
     far_rank = ranks(far_owner, n)
-    raw(1).wait_recv()
+    raw(2).wait_recv()
     fill(far_disp, far_owner, far_rank, far_images)
+    start(4)
     fill(far_shrd, far_shard, far_rank, far_images)
-    start(4)
+    sent(4)
+    landed(4)
     start(5)
-    landed(4)
     align(across)
     route(across, True)
     start(3)
     for way in (0, 1):
         halo(way).wait_send()
-        raw(way).wait_send()
-    for kind in (0, 1, 2, 4, 5):
+    for which in range(3):
+        raw(which).wait_send()
+    for kind in (0, 1, 2, 5):
         sent(kind)
     landed(2)
     landed(5)
@@ -267,8 +270,6 @@
     width = own_rows + 2 * MOST_SENT
     padded_ids = jnp.pad(sent_doc, (MOST_SENT, MOST_SENT), constant_values=-1)
     ids = lax.dynamic_slice_in_dim(padded_ids, me * own_rows, width)[None, :]
-    blank = jnp.zeros((SUB - 3, count), jnp.int32)
-    table = jnp.concatenate([image_owner.T, anchor[None, :], loader_shard.T, blank], axis=0)
     half = jax.ShapeDtypeStruct((rows, feature), jnp.bfloat16)
     slots = pltpu.VMEM((rows, feature), jnp.bfloat16)
     some = pltpu.VMEM((rows // 2, feature), jnp.bfloat16)
@@ -278,21 +279,22 @@
     got_img, got_txt, meta = pl.pallas_call(
         functools.partial(exchange_kernel, n, cap, block, tile),
         out_shape=(half, half, jax.ShapeDtypeStruct((n * SUB, LANES), jnp.int32)),
-        in_specs=[vmem, vmem, vmem, anywhere],
+        in_specs=[vmem] * 5 + [anywhere],
         out_specs=(anywhere, anywhere, vmem),
         scratch_shapes=[
             pltpu.VMEM((width, feature), jnp.bfloat16),
             pltpu.VMEM((count, feature), jnp.bfloat16),
-            pltpu.VMEM((SUB, count), jnp.int32),
+            pltpu.VMEM((1, count), jnp.int32),
+            pltpu.VMEM((1, count), jnp.int32),
             some, some, some, some, slots, slots, slots,
             pltpu.VMEM((n * SUB, LANES), jnp.int32),
             pltpu.VMEM((rows, 1), jnp.int32),
-            dma((7,)), dma((2,)), dma((2,)), dma((2,)), dma((2,)), dma((6, n)), dma((6, n)),
+            dma((7,)), dma((2,)), dma((2,)), dma((3,)), dma((3,)), dma((6, n)), dma((6, n)),
         ],
         compiler_params=pltpu.CompilerParams(
             collective_id=0, has_side_effects=True, vmem_limit_bytes=60 * 1024 * 1024
         ),
-    )(table, images, ids, sentences)
+    )(image_owner.T, anchor[None, :], loader_shard.T, images, ids, sentences)
     if block != cap:
         meta = meta.reshape(n, SUB, LANES)[:, 0, cap + 1]
         picked = got_txt.reshape(n, block, feature)[jnp.maximum(meta - 1, 0), :cap]

time: 102 us -> 101 us (level)
  other arithmetic: 1.38 us -> 0 us
    concatenate x1 -> x0, other arithmetic: 1.38 us -> none  [shards(): jnp.concatenate([image_owner.T, anchor[None, :], loader_shard.T, blank],...]
where the time goes in v3:
time: 101 us; the launch traced here: 100 us
  Pallas kernels  98.4 us (97%)
  local copies, waits for them, and re-layouts  1.42 us (1%)
    pallas_call x1, Pallas kernels, shards(): pl.pallas_call(functools.partial(exchange_kernel, n, cap, block, tile), o...  95 us
    pallas_call x1, Pallas kernels, shards(): pl.pallas_call(functools.partial(place_kernel, n, block, cap + 1), out_sh...  3.36 us

profile of v3, /device:TPU:1, one launch (start us, length us, event | category | flops | bytes accessed | tf_op | source)
XLA Modules:
  0.0 100.5 jit_solution(11247734148503213141)
XLA Ops:
  0.6 0.8 pad_dynamic-slice_fusion
  1.4 0.6 broadcast_in_dim.7.ids_ref
  2.1 95.0 %shard_map.77 = (bf16[512,1280]{1,0:T(8,128)(2,1)}, bf16[512,1280]{1,0:T(8,128)(2,1)}, s32[128,128]{1,0:T(8,128)}) custom-call(s32[1,256]{1,0:T(1,128)} %bitcast.3, s32[1,256]{1,0:T(1,128)} %bitcast.4, s32[1,256]{1,0:T(1,128)} %bitcast.5, bf16[256,1280]{1,0:T(8,128)(2,1)} %images_ref.1, s32[1,2112]{1,0:T(1,128)} %broadcast_in_dim.7.ids_ref, ...), custom_call_target="tpu_custom_call" | custom-call | tf_op jit(solution)/shard_map/pallas_call | solution.py:279
  97.1 3.4 %shard_map.78 = (bf16[512,1280]{1,0:T(8,128)(2,1)}, bf16[512,1280]{1,0:T(8,128)(2,1)}) custom-call(s32[128,128]{1,0:T(8,128)} %get-tuple-element.5.meta_ref, bf16[512,1280]{1,0:T(8,128)(2,1)} %get-tuple-element.6.img_ref, bf16[512,1280]{1,0:T(8,128)(2,1)} %get-tuple-element.7.txt_ref), custom_call_target="tpu_custom_call" | custom-call | tf_op jit(solution)/shard_map/pallas_call | solution.py:304

commit v4 on v3

--- a/solution.py
+++ b/solution.py
@@ -241,21 +241,31 @@
     landed(3)
 
 
-def place_kernel(n, block, lane, meta_ref, img_ref, txt_ref, img_out, txt_out, buf, sems):
-    copy = pltpu.make_async_copy(img_ref, img_out, sems.at[0])
-    copy.start()
+def place_kernel(n, block, lane, meta_ref, img_ref, txt_ref, img_out, txt_out, img_buf, txt_buf, sems):
+    def at(ref, who):
+        return ref.at[pl.ds(pl.multiple_of(who * block, block), block)]
+
+    def picked(s):
+        source = jnp.maximum(meta_ref[s * SUB, lane] - 1, 0)
+        return pltpu.make_async_copy(at(txt_ref, source), at(txt_buf, s), sems.at[1, s])
+
     for s in range(n):
-        source = meta_ref[s * SUB, lane]
-        rows = txt_ref[pl.ds(pl.multiple_of(jnp.maximum(source - 1, 0) * block, block), block), :]
-        buf[pl.ds(s * block, block), :] = jnp.where(source > 0, rows, jnp.zeros_like(rows))
-        pltpu.make_async_copy(
-            buf.at[pl.ds(s * block, block)], txt_out.at[pl.ds(s * block, block)], sems.at[1 + s]
-        ).start()
+        picked(s).start()
+        pltpu.make_async_copy(at(img_ref, s), at(img_buf, s), sems.at[0, s]).start()
     for s in range(n):
-        pltpu.make_async_copy(
-            buf.at[pl.ds(s * block, block)], txt_out.at[pl.ds(s * block, block)], sems.at[1 + s]
-        ).wait()
-    copy.wait()
+        picked(s).wait()
+
+        @pl.when(meta_ref[s * SUB, lane] <= 0)
+        def _():
+            txt_buf[pl.ds(s * block, block), :] = jnp.zeros((block, txt_buf.shape[1]), txt_buf.dtype)
+
+        pltpu.make_async_copy(at(img_ref, s), at(img_buf, s), sems.at[0, s]).wait()
+        pltpu.make_async_copy(at(img_buf, s), at(img_out, s), sems.at[2, s]).start()
+    for s in range(n):
+        pltpu.make_async_copy(at(txt_buf, s), at(txt_out, s), sems.at[3, s]).start()
+    for s in range(n):
+        pltpu.make_async_copy(at(txt_buf, s), at(txt_out, s), sems.at[3, s]).wait()
+        pltpu.make_async_copy(at(img_buf, s), at(img_out, s), sems.at[2, s]).wait()
 
 
 def shards(sentences, sent_doc, images, image_owner, anchor, loader_shard):
@@ -304,9 +314,9 @@
     return pl.pallas_call(
         functools.partial(place_kernel, n, block, cap + 1),
         out_shape=(half, half),
-        in_specs=[pl.BlockSpec(memory_space=pltpu.SMEM), vmem, vmem],
+        in_specs=[pl.BlockSpec(memory_space=pltpu.SMEM), anywhere, anywhere],
         out_specs=(anywhere, anywhere),
-        scratch_shapes=[slots, dma((1 + n,))],
+        scratch_shapes=[slots, slots, dma((4, n))],
     )(meta, got_img, got_txt)
 
 

time: 101 us -> 103 us (1.020)
  Pallas kernels: 98.4 us -> 100 us
    pallas_call x1, Pallas kernels: 3.36 us -> 5.42 us  [shards(): pl.pallas_call(functools.partial(place_kernel, n, block, cap + 1), out_sh...]
where the time goes in v4:
time: 103 us
  Pallas kernels  100 us (97%)
  local copies, waits for them, and re-layouts  1.42 us (1%)
    pallas_call x1, Pallas kernels, shards(): pl.pallas_call(functools.partial(exchange_kernel, n, cap, block, tile), o...  95 us
    pallas_call x1, Pallas kernels, shards(): pl.pallas_call(functools.partial(place_kernel, n, block, cap + 1), out_sh...  5.42 us

profile of v4, /device:TPU:1, one launch (start us, length us, event | category | flops | bytes accessed | tf_op | source)
XLA Modules:
  0.0 102.5 jit_solution(15785420571971193352)
XLA Ops:
  0.6 0.8 pad_dynamic-slice_fusion
  1.4 0.6 broadcast_in_dim.7.ids_ref
  2.1 95.0 %shard_map.77 = (bf16[512,1280]{1,0:T(8,128)(2,1)}, bf16[512,1280]{1,0:T(8,128)(2,1)}, s32[128,128]{1,0:T(8,128)}) custom-call(s32[1,256]{1,0:T(1,128)} %bitcast.3, s32[1,256]{1,0:T(1,128)} %bitcast.4, s32[1,256]{1,0:T(1,128)} %bitcast.5, bf16[256,1280]{1,0:T(8,128)(2,1)} %images_ref.1, s32[1,2112]{1,0:T(1,128)} %broadcast_in_dim.7.ids_ref, ...), custom_call_target="tpu_custom_call" | custom-call | tf_op jit(solution)/shard_map/pallas_call | solution.py:289
  97.1 5.4 %shard_map.78 = (bf16[512,1280]{1,0:T(8,128)(2,1)}, bf16[512,1280]{1,0:T(8,128)(2,1)}) custom-call(s32[128,128]{1,0:T(8,128)} %get-tuple-element.5.meta_ref, bf16[512,1280]{1,0:T(8,128)(2,1)} %get-tuple-element.6.img_ref, bf16[512,1280]{1,0:T(8,128)(2,1)} %get-tuple-element.7.txt_ref), custom_call_target="tpu_custom_call" | custom-call | tf_op jit(solution)/shard_map/pallas_call | solution.py:314
